TPU v7x, 32 devices: a whole 2x2x4 slice. The times are simulated.
32 devices in a mesh: cuts: 2 (over x), wide: 8 (over z, y), batch: 2 (over core).
Axes of the slice: x: 2, y: 2, z: 4, core: 2. Of those that a mesh axis runs over, the one named last changes fastest.
Arguments:
- initial: bfloat16 [2, 64, 2, 2, 256, 256], P('batch', 'cuts', None, None, None, 'wide'), parts along dimension 1, may hold values from -6 to 6
- branches: bfloat16 [8, 2, 2, 256, 2, 256], P(None, None, None, 'batch'), may hold values from -0.1875 to 0.1875
- projectors: float32 [8, 2, 2, 2], replicated, may hold values from -4 to 4
- bits: int32 [2, 8], P('batch'), may hold values from 0 to 1
Outputs:
- amplitudes: float32 [2, 64, 2, 2, 256, 256], P('batch', 'cuts', None, None, 'wide'), parts along dimension 1
There are 2 independent parts, one for each index of `cuts`. A program takes and returns all parts, laid end to end along the dimension named above; an argument that names none is the same for every part. Nothing has to cross between parts.
Inputs may be any that keep to these rules, and one draw needn't show every extreme that they name: `bits`: each entry is a bit.
All inputs are finite; a program needn't handle non-finite values.
Results may differ from a plain program's by a relative error of at most 0.014.
Values may be sent and summed in bfloat16 or wider, within the bound.
A program may use at most 64 MiB of HBM per device.

v0:
```python
import functools

import jax
import jax.numpy as jnp
from jax import lax
from jax.experimental import pallas as pl
from jax.experimental.pallas import tpu as pltpu
from jax.sharding import PartitionSpec as P

MESH = pl.DeviceIdType.MESH
F32 = jnp.float32
BF16 = jnp.bfloat16


def dot(a, b, dims):
    return lax.dot_general(a, b, (dims, ((), ())), preferred_element_type=F32)


def kernel(wide, pair, x_ref, g_ref, proj_ref, bits_ref, out_ref,
           raw, branch, recv1, send2, recv2, state, result, out_sem,
           g_send, g_recv, g_local, s1_sem, r1_sem, l1_sem, s2_sem, r2_sem, l2_sem):
    me = lax.axis_index("wide")
    core = lax.axis_index("batch")
    steps = branch.shape[0]
    cols = recv1.shape[0]
    half = g_ref.shape[3]
    group = branch.shape[4]
    vch, width = recv1.shape[4], recv1.shape[5]
    near = range(1, wide)
    far = sorted(near, key=lambda k: -k.bit_length())

    def partner(k):
        peer, bit = 0, 1
        while bit < wide:
            digit = lax.rem(me // bit, 2)
            peer = peer + bit * (1 - digit if (k // bit) % 2 else digit)
            bit *= 2
        return peer

    barrier = pltpu.get_barrier_semaphore()
    for k in range(1, wide):
        pl.semaphore_signal(barrier, inc=1, device_id={"wide": partner(k)}, device_id_type=MESH)
    for k in range(1, pair):
        pl.semaphore_signal(barrier, inc=1, device_id={"batch": lax.rem(core + k, pair)}, device_id_type=MESH)
    pl.semaphore_wait(barrier, wide + pair - 2)

    def first(j, k):
        peer = partner(k)
        return pltpu.make_async_remote_copy(
            x_ref.at[peer, j], recv1.at[j, me], s1_sem.at[j, k], r1_sem.at[j, k],
            device_id={"wide": peer}, device_id_type=MESH)

    def first_own(j):
        return pltpu.make_async_copy(x_ref.at[me, j], recv1.at[j, me], l1_sem.at[j])

    def second(j, k):
        peer = partner(k)
        return pltpu.make_async_remote_copy(
            send2.at[j, peer], recv2.at[j, me], s2_sem.at[j, k], r2_sem.at[j, k],
            device_id={"wide": peer}, device_id_type=MESH)

    def second_own(j):
        return pltpu.make_async_copy(send2.at[j, me], recv2.at[j, me], l2_sem.at[j])

    def mine(s):
        return raw.at[s, :, :, pl.ds(pl.multiple_of(core * half, half), half)]

    def share(s, k):
        return pltpu.make_async_remote_copy(
            g_ref.at[s], mine(s), g_send.at[s, k], g_recv.at[s, k],
            device_id={"batch": lax.rem(core + k, pair)}, device_id_type=MESH)

    def keep(s):
        return pltpu.make_async_copy(g_ref.at[s], mine(s), g_local.at[s])

    def send_column(j, carry):
        first_own(j).start()
        for k in near:
            first(j, k).start()
        return carry

    for k in far:
        first(0, k).start()
    first_own(0).start()

    def send_branch(s, carry):
        keep(s).start()
        for k in range(1, pair):
            share(s, k).start()
        return carry

    lax.fori_loop(0, steps, send_branch, 0)
    lax.fori_loop(1, cols, send_column, 0)

    def arrive(s, carry):
        keep(s).wait()
        for k in range(1, pair):
            share(s, k).wait_recv()
        for p in range(2):
            for h in range(2):
                both = raw[s, p, h]
                for g in range(2):
                    branch[s, p, g, h] = both[:, g, :]
        return carry
    lax.fori_loop(0, steps, arrive, 0)

    def select(s, g):
        hit = bits_ref[0, s] == 1
        return (jnp.where(hit, proj_ref[4 + g, s], proj_ref[g, s]),
                jnp.where(hit, proj_ref[6 + g, s], proj_ref[2 + g, s]))

    def apply(s, lhs, form, put):
        for g in range(2):
            weight = [branch[s, p, g].reshape(2 * group, width) for p in range(2)]
            if form == "flip":
                prod = [[dot(weight[t], lhs[p], ((0,), (0,))) for t in range(2)] for p in range(2)]
            else:
                axis = 1 if form == "rows" else 0
                prod = [[dot(lhs[p], weight[t], ((axis,), (0,))) for t in range(2)] for p in range(2)]
            re = prod[0][0] - prod[1][1]
            im = prod[0][1] + prod[1][0]
            sr, si = select(s, g)
            put(0, g, sr * re - si * im)
            put(1, g, sr * im + si * re)

    def gathered(buf, j):
        return [jnp.concatenate([buf[j, :, p, h].reshape(wide * vch, width) for h in range(2)], axis=1)
                for p in range(2)]

    def held(slot):
        return [state[slot, p].reshape(2 * group, width) for p in range(2)]

    def column(j, carry):
        for k in near:
            first(j, k).wait_recv()
        first_own(j).wait()

        def put_state(slot):
            def put(p, g, value):
                state[slot, p, g] = value.astype(BF16)
            return put

        apply(0, gathered(recv1, j), "rows", put_state(0))

        def middle(s, carry):
            apply(s, held((s + 1) % 2), "columns", put_state(s % 2))
            return carry

        lax.fori_loop(1, steps - 2, middle, 0)

        def put_send(p, g, value):
            send2[j, :, p, g] = value.astype(BF16).reshape(wide, vch, width)

        apply(steps - 2, held((steps - 3) % 2), "flip", put_send)
        for k in near:
            second(j, k).start()
        second_own(j).start()
        return carry

    lax.fori_loop(0, cols, column, 0)

    def leave(j):
        return pltpu.make_async_copy(result.at[:, j], out_ref.at[:, j], out_sem.at[j])

    def last(j, carry):
        for k in near:
            second(j, k).wait_recv()
        second_own(j).wait()

        def put_out(p, g, value):
            result[:, j, p, g] = value.reshape(wide, vch, width)

        apply(steps - 1, gathered(recv2, j), "rows", put_out)
        leave(j).start()
        return carry

    lax.fori_loop(0, cols, last, 0)

    def drain(j, carry):
        for k in near:
            first(j, k).wait_send()
            second(j, k).wait_send()
        leave(j).wait()
        return carry

    lax.fori_loop(0, cols, drain, 0)

    def drain_branch(s, carry):
        for k in range(1, pair):
            share(s, k).wait_send()
        return carry

    lax.fori_loop(0, steps, drain_branch, 0)


def solution(mesh):
    wide, pair = mesh.shape["wide"], mesh.shape["batch"]

    def shards(initial, branches, projectors, bits):
        _, columns, parts, shared, group, vch = initial.shape
        steps, half, width = branches.shape[0], branches.shape[3], branches.shape[5]
        cols = columns // wide
        x = jnp.swapaxes(initial, 4, 5).reshape(wide, cols, parts, shared, vch, group)
        proj = jnp.transpose(projectors, (1, 2, 3, 0)).reshape(-1, steps)
        dma = pltpu.SemaphoreType.DMA
        chunk = (cols, wide, parts, shared, vch, width)
        chunk_out = (wide, cols, parts, shared, vch, width)
        out = pl.pallas_call(
            functools.partial(kernel, wide, pair),
            out_shape=jax.ShapeDtypeStruct(chunk_out, F32),
            in_specs=[
                pl.BlockSpec(memory_space=pltpu.HBM),
                pl.BlockSpec(memory_space=pltpu.HBM),
                pl.BlockSpec(memory_space=pltpu.SMEM),
                pl.BlockSpec(memory_space=pltpu.SMEM),
            ],
            out_specs=pl.BlockSpec(memory_space=pl.ANY),
            scratch_shapes=[
                pltpu.VMEM((steps, parts, shared, half * pair, shared, width), BF16),
                pltpu.VMEM((steps, parts, shared, shared, half * pair, width), BF16),
                pltpu.VMEM(chunk, BF16),
                pltpu.VMEM(chunk, BF16),
                pltpu.VMEM(chunk, BF16),
                pltpu.VMEM((2, parts, shared, group, width), BF16),
                pltpu.VMEM(chunk_out, F32),
                dma((cols,)),
                dma((steps, pair)), dma((steps, pair)), dma((steps,)),
                dma((cols, wide)), dma((cols, wide)), dma((cols,)),
                dma((cols, wide)), dma((cols, wide)), dma((cols,)),
            ],
            compiler_params=pltpu.CompilerParams(
                collective_id=0, has_side_effects=True, vmem_limit_bytes=44 * 1024 * 1024),
        )(x, branches, proj, bits)
        return out.reshape(1, columns, parts, shared, vch, width)

    in_specs = (
        P("batch", "cuts", None, None, None, "wide"),
        P(None, None, None, "batch", None, None),
        P(),
        P("batch", None),
    )
    out_specs = P("batch", "cuts", None, None, "wide", None)
    return jax.shard_map(shards, mesh=mesh, in_specs=in_specs, out_specs=out_specs, check_vma=False)
```

profile of v0, /device:TPU:14, one launch (start us, length us, event | category | flops | bytes accessed | tf_op | source)
XLA Modules:
  0.0 102.8 jit_solution(12853397090234441640)
XLA Ops:
  0.0 0.0 copy-start
  0.0 1.6 %copy-done = bf16[1,32,2,2,256,32]{4,5,3,2,1,0:T(8,128)(2,1)S(1)} copy-done((bf16[1,32,2,2,256,32]{4,5,3,2,1,0:T(8,128)(2,1)S(1)}, bf16[1,32,2,2,256,32]{4,5,3,2,1,0:T(8,128)(2,1)}, u32[]{:S(2)}) %copy-start) | copy-done | bytes 2097176
  1.6 0.0 copy-start.1
  1.6 0.7 copy-done.1
  2.3 0.0 copy-start.2
  2.3 0.7 copy-done.2
  2.9 97.8 %shard_map.46 = f32[8,4,2,2,32,256]{5,4,3,2,1,0:T(8,128)S(1)} custom-call(bf16[8,4,2,2,32,256]{5,4,3,2,1,0:T(8,128)(2,1)S(1)} %bitcast.8, bf16[8,2,2,128,2,256]{5,4,3,2,1,0:T(2,128)(2,1)} %g_ref.1, f32[8,8]{1,0:T(8,128)S(1)} %bitcast.9, s32[1,8]{1,0:T(1,128)S(1)} %copy-done.2), custom_call_target="tpu_custom_call" | custom-call | tf_op jit(solution)/shard_map/pallas_call | solution.py:208
  100.7 2.0 %copy.6 = f32[1,32,2,2,32,256]{5,4,3,2,1,0:T(8,128)} copy(f32[1,32,2,2,32,256]{5,4,3,2,1,0:T(8,128)S(1)} %bitcast.7) | data formatting | bytes 8388608
Async XLA Ops:
  0.0 1.6 %copy-start = (bf16[1,32,2,2,256,32]{4,5,3,2,1,0:T(8,128)(2,1)S(1)}, bf16[1,32,2,2,256,32]{4,5,3,2,1,0:T(8,128)(2,1)}, u32[]{:S(2)}) copy-start(bf16[1,32,2,2,256,32]{4,5,3,2,1,0:T(8,128)(2,1)} %param.4) | copy-start | bytes 6291460
  1.6 0.7 copy-start.1
  2.3 0.7 copy-start.2
where the time goes:
time: 103 us
  Pallas kernels  97.8 us (95%)
  local copies, waits for them, and re-layouts  4.95 us (5%)
    pallas_call x1, Pallas kernels, shards(): pl.pallas_call(functools.partial(kernel, wide, pair), out_shape=jax.Shape...  97.8 us
    unnamed x7, local copies, waits for them, and re-layouts  4.95 us

commit v1 on v0

--- a/solution.py
+++ b/solution.py
@@ -10,15 +10,17 @@
 MESH = pl.DeviceIdType.MESH
 F32 = jnp.float32
 BF16 = jnp.bfloat16
+SIDE = 2
 
 
 def dot(a, b, dims):
     return lax.dot_general(a, b, (dims, ((), ())), preferred_element_type=F32)
 
 
-def kernel(wide, pair, x_ref, g_ref, proj_ref, bits_ref, out_ref,
-           raw, branch, recv1, send2, recv2, state, result, out_sem,
-           g_send, g_recv, g_local, s1_sem, r1_sem, l1_sem, s2_sem, r2_sem, l2_sem):
+def kernel(wide, pair, x_ref, g_ref, proj_hbm, bits_hbm, out_ref,
+           proj_ref, bits_ref, xs, raw, branch, recv1, send2, recv2, state,
+           c_sem, x_sem, out_sem, g_send, g_recv, g_local,
+           s1_sem, r1_sem, l1_sem, s2_sem, r2_sem, l2_sem, side_sem, know_sem):
     me = lax.axis_index("wide")
     core = lax.axis_index("batch")
     steps = branch.shape[0]
@@ -26,37 +28,72 @@
     half = g_ref.shape[3]
     group = branch.shape[4]
     vch, width = recv1.shape[4], recv1.shape[5]
-    near = range(1, wide)
-    far = sorted(near, key=lambda k: -k.bit_length())
-
-    def partner(k):
-        peer, bit = 0, 1
-        while bit < wide:
-            digit = lax.rem(me // bit, 2)
-            peer = peer + bit * (1 - digit if (k // bit) % 2 else digit)
-            bit *= 2
-        return peer
+
+    rows = wide // SIDE
+    mid = rows // 2
+    row, lane = me // SIDE, me % SIDE
+    low = row < mid
+    inward = jnp.where(low, 1, -1)
+    n_in = jnp.where(low, rows - 1 - row, row)
+    n_out = rows - 1 - n_in
+    middle = n_out == mid - 1
+
+    def device(r, l):
+        return r * SIDE + l
+
+    def signal(sem, dev):
+        pl.semaphore_signal(sem, inc=1, device_id={"wide": dev}, device_id_type=MESH)
+
+    early = 1
+
+    pieces = [(0, early)] + ([(early, cols - early)] if cols > early else [])
+
+    def stage(i):
+        part = pl.ds(*pieces[i])
+        return pltpu.make_async_copy(x_ref.at[:, part], xs.at[:, part], x_sem.at[i])
+
+    consts = [pltpu.make_async_copy(proj_hbm, proj_ref, c_sem.at[0]),
+              pltpu.make_async_copy(bits_hbm, bits_ref, c_sem.at[1])]
 
     barrier = pltpu.get_barrier_semaphore()
-    for k in range(1, wide):
-        pl.semaphore_signal(barrier, inc=1, device_id={"wide": partner(k)}, device_id_type=MESH)
+
+    @pl.when(middle)
+    def _():
+        signal(barrier, device(row + inward, lane))
+
+    @pl.when(n_out > 0)
+    def _():
+        signal(barrier, device(row - inward, lane))
+
+    signal(barrier, device(row, 1 - lane))
     for k in range(1, pair):
         pl.semaphore_signal(barrier, inc=1, device_id={"batch": lax.rem(core + k, pair)}, device_id_type=MESH)
-    pl.semaphore_wait(barrier, wide + pair - 2)
-
-    def first(j, k):
-        peer = partner(k)
-        return pltpu.make_async_remote_copy(
-            x_ref.at[peer, j], recv1.at[j, me], s1_sem.at[j, k], r1_sem.at[j, k],
+    for i in range(len(pieces)):
+        stage(i).start()
+    for c in consts:
+        c.start()
+
+    def first(j, peer):
+        return pltpu.make_async_remote_copy(
+            xs.at[peer, j], recv1.at[j, me], s1_sem.at[j, peer], r1_sem.at[j, me],
+            device_id={"wide": peer}, device_id_type=MESH)
+
+    def first_from(j, peer):
+        return pltpu.make_async_remote_copy(
+            xs.at[peer, j], recv1.at[j, peer], s1_sem.at[j, peer], r1_sem.at[j, peer],
             device_id={"wide": peer}, device_id_type=MESH)
 
     def first_own(j):
         return pltpu.make_async_copy(x_ref.at[me, j], recv1.at[j, me], l1_sem.at[j])
 
-    def second(j, k):
-        peer = partner(k)
-        return pltpu.make_async_remote_copy(
-            send2.at[j, peer], recv2.at[j, me], s2_sem.at[j, k], r2_sem.at[j, k],
+    def second(j, peer):
+        return pltpu.make_async_remote_copy(
+            send2.at[j, peer], recv2.at[j, me], s2_sem.at[j, peer], r2_sem.at[j, me],
+            device_id={"wide": peer}, device_id_type=MESH)
+
+    def second_from(j, peer):
+        return pltpu.make_async_remote_copy(
+            send2.at[j, peer], recv2.at[j, peer], s2_sem.at[j, peer], r2_sem.at[j, peer],
             device_id={"wide": peer}, device_id_type=MESH)
 
     def second_own(j):
@@ -73,15 +110,33 @@
     def keep(s):
         return pltpu.make_async_copy(g_ref.at[s], mine(s), g_local.at[s])
 
-    def send_column(j, carry):
-        first_own(j).start()
-        for k in near:
-            first(j, k).start()
-        return carry
-
-    for k in far:
-        first(0, k).start()
-    first_own(0).start()
+    def ordered():
+        base = jnp.where(low, 0, mid)
+        peers = [device(row, 1 - lane)]
+        for i in range(1, mid):
+            r = base + lax.rem(row - base + i, mid)
+            peers += [device(r, lane), device(r, 1 - lane)]
+        for i in range(mid):
+            r = jnp.where(low, rows - 1 - i, i)
+            peers += [device(r, lane), device(r, 1 - lane)]
+        return peers
+
+    peers = ordered()
+
+    def first_to(peer, start, stop):
+        for j in range(start, stop):
+            first(j, peer).start()
+
+    pl.semaphore_wait(barrier, pair + 1)
+    signal(side_sem, device(row, 1 - lane))
+
+    @pl.when(jnp.logical_not(middle))
+    def _():
+        signal(know_sem.at[0, 0], device(row + inward, lane))
+
+    stage(0).wait()
+    first_to(device(row + inward, lane), 0, early)
+    first_to(device(row, 1 - lane), 0, early)
 
     def send_branch(s, carry):
         keep(s).start()
@@ -90,7 +145,61 @@
         return carry
 
     lax.fori_loop(0, steps, send_branch, 0)
-    lax.fori_loop(1, cols, send_column, 0)
+    for j in range(cols):
+        first_own(j).start()
+
+    pl.semaphore_wait(side_sem, 1)
+    first_to(device(row + inward, 1 - lane), 0, early)
+
+    @pl.when(n_out > 0)
+    def _():
+        pl.semaphore_wait(know_sem.at[0, 0], 1)
+
+        @pl.when(n_in > 0)
+        def _():
+            signal(know_sem.at[1, 1], device(row - inward, lane))
+            for l in range(SIDE):
+                first_to(device(row - inward, l), 0, early)
+
+    def tell_in(d):
+        @pl.when(middle)
+        def _():
+            signal(know_sem.at[1, d], device(row + inward, lane))
+
+        @pl.when(jnp.logical_not(middle))
+        def _():
+            signal(know_sem.at[0, d], device(row + inward, lane))
+
+    @pl.when(n_out > 0)
+    def _():
+        tell_in(1)
+
+    for d in range(2, rows):
+        @pl.when(n_in >= d)
+        def _():
+            pl.semaphore_wait(know_sem.at[1, d - 1], 1)
+
+            @pl.when(n_out > 0)
+            def _():
+                signal(know_sem.at[1, d], device(row - inward, lane))
+            for l in range(SIDE):
+                first_to(device(row + d * inward, l), 0, early)
+
+        @pl.when(n_out >= d)
+        def _():
+            pl.semaphore_wait(know_sem.at[0, d - 1], 1)
+            tell_in(d)
+            for l in range(SIDE):
+                first_to(device(row - d * inward, l), 0, early)
+
+    for i in range(1, len(pieces)):
+        stage(i).wait()
+    for j in range(early, cols):
+        for p in peers:
+            first(j, p).start()
+
+    for c in consts:
+        c.wait()
 
     def arrive(s, carry):
         keep(s).wait()
@@ -127,12 +236,17 @@
         return [jnp.concatenate([buf[j, :, p, h].reshape(wide * vch, width) for h in range(2)], axis=1)
                 for p in range(2)]
 
+    def gathered_part(buf, j, start, count):
+        part = pl.ds(start, count)
+        return [jnp.concatenate([buf[j, part, p, h].reshape(count * vch, width) for h in range(2)], axis=1)
+                for p in range(2)]
+
     def held(slot):
         return [state[slot, p].reshape(2 * group, width) for p in range(2)]
 
     def column(j, carry):
-        for k in near:
-            first(j, k).wait_recv()
+        for p in peers:
+            first_from(j, p).wait_recv()
         first_own(j).wait()
 
         def put_state(slot):
@@ -142,45 +256,40 @@
 
         apply(0, gathered(recv1, j), "rows", put_state(0))
 
-        def middle(s, carry):
+        def middle_step(s, carry):
             apply(s, held((s + 1) % 2), "columns", put_state(s % 2))
             return carry
 
-        lax.fori_loop(1, steps - 2, middle, 0)
+        lax.fori_loop(1, steps - 2, middle_step, 0)
 
         def put_send(p, g, value):
             send2[j, :, p, g] = value.astype(BF16).reshape(wide, vch, width)
 
         apply(steps - 2, held((steps - 3) % 2), "flip", put_send)
-        for k in near:
-            second(j, k).start()
+        for p in peers:
+            second(j, p).start()
         second_own(j).start()
         return carry
 
     lax.fori_loop(0, cols, column, 0)
 
-    def leave(j):
-        return pltpu.make_async_copy(result.at[:, j], out_ref.at[:, j], out_sem.at[j])
-
     def last(j, carry):
-        for k in near:
-            second(j, k).wait_recv()
+        for p in peers:
+            second_from(j, p).wait_recv()
         second_own(j).wait()
 
         def put_out(p, g, value):
-            result[:, j, p, g] = value.reshape(wide, vch, width)
+            out_ref[:, j, p, g] = value.reshape(wide, vch, width)
 
         apply(steps - 1, gathered(recv2, j), "rows", put_out)
-        leave(j).start()
         return carry
 
     lax.fori_loop(0, cols, last, 0)
 
     def drain(j, carry):
-        for k in near:
-            first(j, k).wait_send()
-            second(j, k).wait_send()
-        leave(j).wait()
+        for p in peers:
+            first(j, p).wait_send()
+            second(j, p).wait_send()
         return carry
 
     lax.fori_loop(0, cols, drain, 0)
@@ -208,29 +317,28 @@
         out = pl.pallas_call(
             functools.partial(kernel, wide, pair),
             out_shape=jax.ShapeDtypeStruct(chunk_out, F32),
-            in_specs=[
-                pl.BlockSpec(memory_space=pltpu.HBM),
-                pl.BlockSpec(memory_space=pltpu.HBM),
-                pl.BlockSpec(memory_space=pltpu.SMEM),
-                pl.BlockSpec(memory_space=pltpu.SMEM),
-            ],
-            out_specs=pl.BlockSpec(memory_space=pl.ANY),
+            in_specs=[pl.BlockSpec(memory_space=pltpu.HBM)] * 4,
+            out_specs=pl.BlockSpec(memory_space=pltpu.VMEM),
             scratch_shapes=[
+                pltpu.SMEM(proj.shape, F32),
+                pltpu.SMEM(bits.shape, jnp.int32),
+                pltpu.VMEM(x.shape, BF16),
                 pltpu.VMEM((steps, parts, shared, half * pair, shared, width), BF16),
                 pltpu.VMEM((steps, parts, shared, shared, half * pair, width), BF16),
                 pltpu.VMEM(chunk, BF16),
                 pltpu.VMEM(chunk, BF16),
                 pltpu.VMEM(chunk, BF16),
                 pltpu.VMEM((2, parts, shared, group, width), BF16),
-                pltpu.VMEM(chunk_out, F32),
-                dma((cols,)),
+                dma((2,)), dma((2,)), dma((cols,)),
                 dma((steps, pair)), dma((steps, pair)), dma((steps,)),
                 dma((cols, wide)), dma((cols, wide)), dma((cols,)),
                 dma((cols, wide)), dma((cols, wide)), dma((cols,)),
+                pltpu.SemaphoreType.REGULAR,
+                pltpu.SemaphoreType.REGULAR((2, wide // SIDE)),
             ],
             compiler_params=pltpu.CompilerParams(
                 collective_id=0, has_side_effects=True, vmem_limit_bytes=44 * 1024 * 1024),
-        )(x, branches, proj, bits)
+        )(*(pltpu.with_memory_space_constraint(a, pltpu.HBM) for a in (x, branches, proj, bits)))
         return out.reshape(1, columns, parts, shared, vch, width)
 
     in_specs = (

time: 103 us -> 99.6 us (0.967); the launches traced: 103 us -> 98.1 us
  local copies, waits for them, and re-layouts: 4.95 us -> 2.02 us
  Pallas kernels: 97.8 us -> 96 us
    unnamed x7 -> x1, local copies, waits for them, and re-layouts: 4.95 us -> 2.02 us
    pallas_call x1, Pallas kernels: 97.8 us -> 96 us  [shards(): pl.pallas_call(functools.partial(kernel, wide, pair), out_shape=jax.Shape...]
where the time goes in v1:
time: 99.6 us; the launch traced here: 98.1 us
  Pallas kernels  96 us (96%)
  local copies, waits for them, and re-layouts  2.02 us (2%)
    pallas_call x1, Pallas kernels, shards(): pl.pallas_call(functools.partial(kernel, wide, pair), out_shape=jax.Shape...  96 us
    unnamed x1, local copies, waits for them, and re-layouts  2.02 us

profile of v1, /device:TPU:14, one launch (start us, length us, event | category | flops | bytes accessed | tf_op | source)
XLA Modules:
  0.0 98.1 jit_solution(439884392368495558)
XLA Ops:
  0.0 96.0 %shard_map.46 = f32[8,4,2,2,32,256]{5,4,3,2,1,0:T(8,128)S(1)} custom-call(bf16[8,4,2,2,32,256]{5,4,3,2,1,0:T(8,128)(2,1)} %bitcast.8, bf16[8,2,2,128,2,256]{5,4,3,2,1,0:T(2,128)(2,1)} %g_ref.1, f32[8,8]{1,0:T(8,128)} %bitcast.9, s32[1,8]{1,0:T(1,128)} %bits_hbm.1), custom_call_target="tpu_custom_call" | custom-call | tf_op jit(solution)/shard_map/pallas_call | solution.py:317
  96.0 2.0 %copy.6 = f32[1,32,2,2,32,256]{5,4,3,2,1,0:T(8,128)} copy(f32[1,32,2,2,32,256]{5,4,3,2,1,0:T(8,128)S(1)} %bitcast.7) | data formatting | bytes 8388608

commit v2 on v1

--- a/solution.py
+++ b/solution.py
@@ -1,4 +1,5 @@
 import functools
+import math
 
 import jax
 import jax.numpy as jnp
@@ -19,8 +20,7 @@
 
 def kernel(wide, pair, x_ref, g_ref, proj_hbm, bits_hbm, out_ref,
            proj_ref, bits_ref, xs, raw, branch, recv1, send2, recv2, state,
-           c_sem, x_sem, out_sem, g_send, g_recv, g_local,
-           s1_sem, r1_sem, l1_sem, s2_sem, r2_sem, l2_sem, side_sem, know_sem):
+           c_sem, x_sem, g_out, g_in, s1_sem, r1_sem, s2_sem, r2_sem, side_sem, out_know, in_know):
     me = lax.axis_index("wide")
     core = lax.axis_index("batch")
     steps = branch.shape[0]
@@ -44,13 +44,8 @@
     def signal(sem, dev):
         pl.semaphore_signal(sem, inc=1, device_id={"wide": dev}, device_id_type=MESH)
 
-    early = 1
-
-    pieces = [(0, early)] + ([(early, cols - early)] if cols > early else [])
-
-    def stage(i):
-        part = pl.ds(*pieces[i])
-        return pltpu.make_async_copy(x_ref.at[:, part], xs.at[:, part], x_sem.at[i])
+    def stage(l):
+        return pltpu.make_async_copy(x_ref.at[device(row + inward, l), 0], xs.at[l], x_sem)
 
     consts = [pltpu.make_async_copy(proj_hbm, proj_ref, c_sem.at[0]),
               pltpu.make_async_copy(bits_hbm, bits_ref, c_sem.at[1])]
@@ -68,47 +63,39 @@
     signal(barrier, device(row, 1 - lane))
     for k in range(1, pair):
         pl.semaphore_signal(barrier, inc=1, device_id={"batch": lax.rem(core + k, pair)}, device_id_type=MESH)
-    for i in range(len(pieces)):
-        stage(i).start()
+    for l in range(SIDE):
+        stage(l).start()
     for c in consts:
         c.start()
 
-    def first(j, peer):
+    def filled(ref, sem):
+        pltpu.make_async_copy(ref, ref, sem).wait()
+
+    def first(j, peer, src=None):
         return pltpu.make_async_remote_copy(
-            xs.at[peer, j], recv1.at[j, me], s1_sem.at[j, peer], r1_sem.at[j, me],
+            x_ref.at[peer, j] if src is None else src, recv1.at[j, me], s1_sem, r1_sem.at[j],
             device_id={"wide": peer}, device_id_type=MESH)
 
-    def first_from(j, peer):
-        return pltpu.make_async_remote_copy(
-            xs.at[peer, j], recv1.at[j, peer], s1_sem.at[j, peer], r1_sem.at[j, peer],
-            device_id={"wide": peer}, device_id_type=MESH)
-
     def first_own(j):
-        return pltpu.make_async_copy(x_ref.at[me, j], recv1.at[j, me], l1_sem.at[j])
+        return pltpu.make_async_copy(x_ref.at[me, j], recv1.at[j, me], r1_sem.at[j])
 
     def second(j, peer):
         return pltpu.make_async_remote_copy(
-            send2.at[j, peer], recv2.at[j, me], s2_sem.at[j, peer], r2_sem.at[j, me],
+            send2.at[j, peer], recv2.at[j, me], s2_sem, r2_sem.at[j],
             device_id={"wide": peer}, device_id_type=MESH)
 
-    def second_from(j, peer):
-        return pltpu.make_async_remote_copy(
-            send2.at[j, peer], recv2.at[j, peer], s2_sem.at[j, peer], r2_sem.at[j, peer],
-            device_id={"wide": peer}, device_id_type=MESH)
-
-    def second_own(j):
-        return pltpu.make_async_copy(send2.at[j, me], recv2.at[j, me], l2_sem.at[j])
+    batch = steps // g_in.shape[0]
 
     def mine(s):
         return raw.at[s, :, :, pl.ds(pl.multiple_of(core * half, half), half)]
 
     def share(s, k):
         return pltpu.make_async_remote_copy(
-            g_ref.at[s], mine(s), g_send.at[s, k], g_recv.at[s, k],
+            g_ref.at[s], mine(s), g_out, g_in.at[s // batch],
             device_id={"batch": lax.rem(core + k, pair)}, device_id_type=MESH)
 
     def keep(s):
-        return pltpu.make_async_copy(g_ref.at[s], mine(s), g_local.at[s])
+        return pltpu.make_async_copy(g_ref.at[s], mine(s), g_in.at[s // batch])
 
     def ordered():
         base = jnp.where(low, 0, mid)
@@ -123,20 +110,22 @@
 
     peers = ordered()
 
-    def first_to(peer, start, stop):
-        for j in range(start, stop):
-            first(j, peer).start()
-
     pl.semaphore_wait(barrier, pair + 1)
     signal(side_sem, device(row, 1 - lane))
 
     @pl.when(jnp.logical_not(middle))
     def _():
-        signal(know_sem.at[0, 0], device(row + inward, lane))
-
-    stage(0).wait()
-    first_to(device(row + inward, lane), 0, early)
-    first_to(device(row, 1 - lane), 0, early)
+        signal(out_know.at[0], device(row + inward, lane))
+
+    def first_inward(l):
+        for i in range(SIDE):
+            @pl.when(lane == (i if l == 0 else 1 - i))
+            def _():
+                first(0, device(row + inward, i), xs.at[i]).start()
+
+    filled(xs, x_sem)
+    first_inward(0)
+    first(0, device(row, 1 - lane)).start()
 
     def send_branch(s, carry):
         keep(s).start()
@@ -149,26 +138,27 @@
         first_own(j).start()
 
     pl.semaphore_wait(side_sem, 1)
-    first_to(device(row + inward, 1 - lane), 0, early)
+    first_inward(1)
 
     @pl.when(n_out > 0)
     def _():
-        pl.semaphore_wait(know_sem.at[0, 0], 1)
+        pl.semaphore_wait(out_know.at[0], 1)
 
         @pl.when(n_in > 0)
         def _():
-            signal(know_sem.at[1, 1], device(row - inward, lane))
+            signal(in_know.at[0], device(row - inward, lane))
             for l in range(SIDE):
-                first_to(device(row - inward, l), 0, early)
+                first(0, device(row - inward, l)).start()
 
     def tell_in(d):
         @pl.when(middle)
         def _():
-            signal(know_sem.at[1, d], device(row + inward, lane))
-
-        @pl.when(jnp.logical_not(middle))
-        def _():
-            signal(know_sem.at[0, d], device(row + inward, lane))
+            signal(in_know.at[d - 1], device(row + inward, lane))
+
+        if d < mid - 1:
+            @pl.when(jnp.logical_not(middle))
+            def _():
+                signal(out_know.at[d], device(row + inward, lane))
 
     @pl.when(n_out > 0)
     def _():
@@ -177,24 +167,23 @@
     for d in range(2, rows):
         @pl.when(n_in >= d)
         def _():
-            pl.semaphore_wait(know_sem.at[1, d - 1], 1)
-
-            @pl.when(n_out > 0)
+            pl.semaphore_wait(in_know.at[d - 2], 1)
+            if d < rows - 1:
+                @pl.when(n_out > 0)
+                def _():
+                    signal(in_know.at[d - 1], device(row - inward, lane))
+            for l in range(SIDE):
+                first(0, device(row + d * inward, l)).start()
+
+        if d < mid:
+            @pl.when(n_out >= d)
             def _():
-                signal(know_sem.at[1, d], device(row - inward, lane))
-            for l in range(SIDE):
-                first_to(device(row + d * inward, l), 0, early)
-
-        @pl.when(n_out >= d)
-        def _():
-            pl.semaphore_wait(know_sem.at[0, d - 1], 1)
-            tell_in(d)
-            for l in range(SIDE):
-                first_to(device(row - d * inward, l), 0, early)
-
-    for i in range(1, len(pieces)):
-        stage(i).wait()
-    for j in range(early, cols):
+                pl.semaphore_wait(out_know.at[d - 1], 1)
+                tell_in(d)
+                for l in range(SIDE):
+                    first(0, device(row - d * inward, l)).start()
+
+    for j in range(1, cols):
         for p in peers:
             first(j, p).start()
 
@@ -202,9 +191,9 @@
         c.wait()
 
     def arrive(s, carry):
-        keep(s).wait()
-        for k in range(1, pair):
-            share(s, k).wait_recv()
+        @pl.when(lax.rem(s, batch) == 0)
+        def _():
+            filled(raw.at[pl.ds(s, batch)], g_in.at[s // batch])
         for p in range(2):
             for h in range(2):
                 both = raw[s, p, h]
@@ -245,9 +234,7 @@
         return [state[slot, p].reshape(2 * group, width) for p in range(2)]
 
     def column(j, carry):
-        for p in peers:
-            first_from(j, p).wait_recv()
-        first_own(j).wait()
+        filled(recv1.at[j], r1_sem.at[j])
 
         def put_state(slot):
             def put(p, g, value):
@@ -268,15 +255,13 @@
         apply(steps - 2, held((steps - 3) % 2), "flip", put_send)
         for p in peers:
             second(j, p).start()
-        second_own(j).start()
+        recv2[j, me] = send2[j, me]
         return carry
 
     lax.fori_loop(0, cols, column, 0)
 
     def last(j, carry):
-        for p in peers:
-            second_from(j, p).wait_recv()
-        second_own(j).wait()
+        filled(recv2.at[j, pl.ds(0, wide - 1)], r2_sem.at[j])
 
         def put_out(p, g, value):
             out_ref[:, j, p, g] = value.reshape(wide, vch, width)
@@ -286,20 +271,10 @@
 
     lax.fori_loop(0, cols, last, 0)
 
-    def drain(j, carry):
-        for p in peers:
-            first(j, p).wait_send()
-            second(j, p).wait_send()
-        return carry
-
-    lax.fori_loop(0, cols, drain, 0)
-
-    def drain_branch(s, carry):
-        for k in range(1, pair):
-            share(s, k).wait_send()
-        return carry
-
-    lax.fori_loop(0, steps, drain_branch, 0)
+    filled(send2.at[:, pl.ds(0, wide - 1)], s1_sem)
+    filled(send2.at[:, pl.ds(0, wide - 1)], s2_sem)
+    for k in range(1, pair):
+        filled(raw.at[:, :, :, pl.ds(0, half)], g_out)
 
 
 def solution(mesh):
@@ -322,19 +297,18 @@
             scratch_shapes=[
                 pltpu.SMEM(proj.shape, F32),
                 pltpu.SMEM(bits.shape, jnp.int32),
-                pltpu.VMEM(x.shape, BF16),
+                pltpu.VMEM((SIDE,) + x.shape[2:], BF16),
                 pltpu.VMEM((steps, parts, shared, half * pair, shared, width), BF16),
                 pltpu.VMEM((steps, parts, shared, shared, half * pair, width), BF16),
                 pltpu.VMEM(chunk, BF16),
                 pltpu.VMEM(chunk, BF16),
                 pltpu.VMEM(chunk, BF16),
                 pltpu.VMEM((2, parts, shared, group, width), BF16),
-                dma((2,)), dma((2,)), dma((cols,)),
-                dma((steps, pair)), dma((steps, pair)), dma((steps,)),
-                dma((cols, wide)), dma((cols, wide)), dma((cols,)),
-                dma((cols, wide)), dma((cols, wide)), dma((cols,)),
+                dma((2,)), dma(()), dma(()), dma((math.gcd(2, steps),)),
+                dma(()), dma((cols,)), dma(()), dma((cols,)),
                 pltpu.SemaphoreType.REGULAR,
-                pltpu.SemaphoreType.REGULAR((2, wide // SIDE)),
+                pltpu.SemaphoreType.REGULAR((wide // SIDE // 2 - 1,)),
+                pltpu.SemaphoreType.REGULAR((wide // SIDE - 2,)),
             ],
             compiler_params=pltpu.CompilerParams(
                 collective_id=0, has_side_effects=True, vmem_limit_bytes=44 * 1024 * 1024),

time: 99.6 us -> 97.7 us (0.981)
  Pallas kernels: 96 us -> 94.3 us
    pallas_call x1, Pallas kernels: 96 us -> 94.3 us  [shards(): pl.pallas_call(functools.partial(kernel, wide, pair), out_shape=jax.Shape...]
where the time goes in v2:
time: 97.7 us; the launch traced here: 96.3 us
  Pallas kernels  94.3 us (97%)
  local copies, waits for them, and re-layouts  2.02 us (2%)
    pallas_call x1, Pallas kernels, shards(): pl.pallas_call(functools.partial(kernel, wide, pair), out_shape=jax.Shape...  94.3 us
    unnamed x1, local copies, waits for them, and re-layouts  2.02 us

profile of v2, /device:TPU:14, one launch (start us, length us, event | category | flops | bytes accessed | tf_op | source)
XLA Modules:
  0.0 96.3 jit_solution(9478283230105584940)
XLA Ops:
  0.0 94.3 %shard_map.46 = f32[8,4,2,2,32,256]{5,4,3,2,1,0:T(8,128)S(1)} custom-call(bf16[8,4,2,2,32,256]{5,4,3,2,1,0:T(8,128)(2,1)} %bitcast.8, bf16[8,2,2,128,2,256]{5,4,3,2,1,0:T(2,128)(2,1)} %g_ref.1, f32[8,8]{1,0:T(8,128)} %bitcast.9, s32[1,8]{1,0:T(1,128)} %bits_hbm.1), custom_call_target="tpu_custom_call" | custom-call | tf_op jit(solution)/shard_map/pallas_call | solution.py:292
  94.3 2.0 %copy.6 = f32[1,32,2,2,32,256]{5,4,3,2,1,0:T(8,128)} copy(f32[1,32,2,2,32,256]{5,4,3,2,1,0:T(8,128)S(1)} %bitcast.7) | data formatting | bytes 8388608

commit v3 on v2

--- a/solution.py
+++ b/solution.py
@@ -50,6 +50,9 @@
     consts = [pltpu.make_async_copy(proj_hbm, proj_ref, c_sem.at[0]),
               pltpu.make_async_copy(bits_hbm, bits_ref, c_sem.at[1])]
 
+    for l in range(SIDE):
+        stage(l).start()
+
     barrier = pltpu.get_barrier_semaphore()
 
     @pl.when(middle)
@@ -60,11 +63,11 @@
     def _():
         signal(barrier, device(row - inward, lane))
 
-    signal(barrier, device(row, 1 - lane))
+    @pl.when(lane == 0)
+    def _():
+        signal(barrier, device(row, 1))
     for k in range(1, pair):
         pl.semaphore_signal(barrier, inc=1, device_id={"batch": lax.rem(core + k, pair)}, device_id_type=MESH)
-    for l in range(SIDE):
-        stage(l).start()
     for c in consts:
         c.start()
 
@@ -79,9 +82,9 @@
     def first_own(j):
         return pltpu.make_async_copy(x_ref.at[me, j], recv1.at[j, me], r1_sem.at[j])
 
-    def second(j, peer):
+    def second(j, peer, arrived):
         return pltpu.make_async_remote_copy(
-            send2.at[j, peer], recv2.at[j, me], s2_sem, r2_sem.at[j],
+            send2.at[j, peer], recv2.at[j, me], s2_sem, r2_sem.at[arrived],
             device_id={"wide": peer}, device_id_type=MESH)
 
     batch = steps // g_in.shape[0]
@@ -104,18 +107,21 @@
             r = base + lax.rem(row - base + i, mid)
             peers += [device(r, lane), device(r, 1 - lane)]
         for i in range(mid):
-            r = jnp.where(low, rows - 1 - i, i)
-            peers += [device(r, lane), device(r, 1 - lane)]
+            r = jnp.where(low, mid + i, i)
+            peers += [device(r, l) for l in range(SIDE)]
         return peers
 
     peers = ordered()
-
-    pl.semaphore_wait(barrier, pair + 1)
-    signal(side_sem, device(row, 1 - lane))
-
-    @pl.when(jnp.logical_not(middle))
-    def _():
-        signal(out_know.at[0], device(row + inward, lane))
+    near = mid * SIDE - 1
+
+    @pl.when(lane == 0)
+    def _():
+        pl.semaphore_wait(barrier, pair)
+
+    @pl.when(lane == 1)
+    def _():
+        pl.semaphore_wait(barrier, pair + 1)
+        signal(side_sem, device(row, 0))
 
     def first_inward(l):
         for i in range(SIDE):
@@ -125,7 +131,8 @@
 
     filled(xs, x_sem)
     first_inward(0)
-    first(0, device(row, 1 - lane)).start()
+    for j in range(1, min(cols, 2)):
+        first(j, device(row + inward, lane)).start()
 
     def send_branch(s, carry):
         keep(s).start()
@@ -138,6 +145,16 @@
         first_own(j).start()
 
     pl.semaphore_wait(side_sem, 1)
+
+    @pl.when(lane == 0)
+    def _():
+        signal(side_sem, device(row, 1))
+
+    @pl.when(jnp.logical_not(middle))
+    def _():
+        signal(out_know.at[0], device(row + inward, lane))
+
+    first(0, device(row, 1 - lane)).start()
     first_inward(1)
 
     @pl.when(n_out > 0)
@@ -185,7 +202,12 @@
 
     for j in range(1, cols):
         for p in peers:
-            first(j, p).start()
+            if j < 2:
+                @pl.when(p != device(row + inward, lane))
+                def _():
+                    first(j, p).start()
+            else:
+                first(j, p).start()
 
     for c in consts:
         c.wait()
@@ -221,11 +243,7 @@
             put(0, g, sr * re - si * im)
             put(1, g, sr * im + si * re)
 
-    def gathered(buf, j):
-        return [jnp.concatenate([buf[j, :, p, h].reshape(wide * vch, width) for h in range(2)], axis=1)
-                for p in range(2)]
-
-    def gathered_part(buf, j, start, count):
+    def gathered(buf, j, start, count):
         part = pl.ds(start, count)
         return [jnp.concatenate([buf[j, part, p, h].reshape(count * vch, width) for h in range(2)], axis=1)
                 for p in range(2)]
@@ -241,7 +259,7 @@
                 state[slot, p, g] = value.astype(BF16)
             return put
 
-        apply(0, gathered(recv1, j), "rows", put_state(0))
+        apply(0, gathered(recv1, j, 0, wide), "rows", put_state(0))
 
         def middle_step(s, carry):
             apply(s, held((s + 1) % 2), "columns", put_state(s % 2))
@@ -253,23 +271,31 @@
             send2[j, :, p, g] = value.astype(BF16).reshape(wide, vch, width)
 
         apply(steps - 2, held((steps - 3) % 2), "flip", put_send)
-        for p in peers:
-            second(j, p).start()
+        final = (j == cols - 1).astype(jnp.int32)
+        for i, p in enumerate(peers):
+            second(j, p, j + final if i >= near else j).start()
         recv2[j, me] = send2[j, me]
         return carry
 
     lax.fori_loop(0, cols, column, 0)
 
+    def finish(j, start, count):
+        def put_out(p, g, value):
+            out_ref[pl.ds(start, count), j, p, g] = value.reshape(count, vch, width)
+
+        apply(steps - 1, gathered(recv2, j, start, count), "rows", put_out)
+
     def last(j, carry):
         filled(recv2.at[j, pl.ds(0, wide - 1)], r2_sem.at[j])
-
-        def put_out(p, g, value):
-            out_ref[:, j, p, g] = value.reshape(wide, vch, width)
-
-        apply(steps - 1, gathered(recv2, j), "rows", put_out)
+        finish(j, 0, wide)
         return carry
 
-    lax.fori_loop(0, cols, last, 0)
+    lax.fori_loop(0, cols - 1, last, 0)
+    here = jnp.where(low, 0, near + 1)
+    filled(recv2.at[cols - 1, pl.ds(0, near)], r2_sem.at[cols - 1])
+    finish(cols - 1, here, near + 1)
+    filled(recv2.at[cols - 1, pl.ds(0, near + 1)], r2_sem.at[cols])
+    finish(cols - 1, near + 1 - here, near + 1)
 
     filled(send2.at[:, pl.ds(0, wide - 1)], s1_sem)
     filled(send2.at[:, pl.ds(0, wide - 1)], s2_sem)
@@ -305,7 +331,7 @@
                 pltpu.VMEM(chunk, BF16),
                 pltpu.VMEM((2, parts, shared, group, width), BF16),
                 dma((2,)), dma(()), dma(()), dma((math.gcd(2, steps),)),
-                dma(()), dma((cols,)), dma(()), dma((cols,)),
+                dma(()), dma((cols,)), dma(()), dma((cols + 1,)),
                 pltpu.SemaphoreType.REGULAR,
                 pltpu.SemaphoreType.REGULAR((wide // SIDE // 2 - 1,)),
                 pltpu.SemaphoreType.REGULAR((wide // SIDE - 2,)),

time: 97.7 us -> 96.2 us (0.985); the launches traced: 96.3 us -> 95.8 us
  no operation moved by 1% of the time
where the time goes in v3:
time: 96.2 us; the launch traced here: 95.8 us
  Pallas kernels  93.8 us (98%)
  local copies, waits for them, and re-layouts  2.02 us (2%)
    pallas_call x1, Pallas kernels, shards(): pl.pallas_call(functools.partial(kernel, wide, pair), out_shape=jax.Shape...  93.8 us
    unnamed x1, local copies, waits for them, and re-layouts  2.02 us

profile of v3, /device:TPU:14, one launch (start us, length us, event | category | flops | bytes accessed | tf_op | source)
XLA Modules:
  0.0 95.8 jit_solution(9967479538285441383)
XLA Ops:
  0.0 93.8 %shard_map.46 = f32[8,4,2,2,32,256]{5,4,3,2,1,0:T(8,128)S(1)} custom-call(bf16[8,4,2,2,32,256]{5,4,3,2,1,0:T(8,128)(2,1)} %bitcast.8, bf16[8,2,2,128,2,256]{5,4,3,2,1,0:T(2,128)(2,1)} %g_ref.1, f32[8,8]{1,0:T(8,128)} %bitcast.9, s32[1,8]{1,0:T(1,128)} %bits_hbm.1), custom_call_target="tpu_custom_call" | custom-call | tf_op jit(solution)/shard_map/pallas_call | solution.py:318
  93.8 2.0 %copy.6 = f32[1,32,2,2,32,256]{5,4,3,2,1,0:T(8,128)} copy(f32[1,32,2,2,32,256]{5,4,3,2,1,0:T(8,128)S(1)} %bitcast.7) | data formatting | bytes 8388608

commit v4 on v3

--- a/solution.py
+++ b/solution.py
@@ -271,9 +271,33 @@
             send2[j, :, p, g] = value.astype(BF16).reshape(wide, vch, width)
 
         apply(steps - 2, held((steps - 3) % 2), "flip", put_send)
-        final = (j == cols - 1).astype(jnp.int32)
-        for i, p in enumerate(peers):
-            second(j, p, j + final if i >= near else j).start()
+        for p in peers[:near]:
+            second(j, p, j).start()
+        across = peers[near:]
+        split = len(across) // 2 if cols > 1 else len(across)
+
+        @pl.when(j < cols - 2)
+        def _():
+            for p in across:
+                second(j, p, j).start()
+
+        if cols > 1:
+            @pl.when(j == cols - 2)
+            def _():
+                for p in across[:split]:
+                    second(j, p, j).start()
+
+        @pl.when(j == cols - 1)
+        def _():
+            second(j, across[0], cols).start()
+            for p in across[split:-1]:
+                second(j - 1, p, j - 1).start()
+            for p in across[1:-1]:
+                second(j, p, cols).start()
+            for p in across[split:][-1:]:
+                second(j - 1, p, j - 1).start()
+            second(j, across[-1], cols).start()
+
         recv2[j, me] = send2[j, me]
         return carry
 
@@ -290,10 +314,21 @@
         finish(j, 0, wide)
         return carry
 
-    lax.fori_loop(0, cols - 1, last, 0)
     here = jnp.where(low, 0, near + 1)
-    filled(recv2.at[cols - 1, pl.ds(0, near)], r2_sem.at[cols - 1])
-    finish(cols - 1, here, near + 1)
+
+    def finish_near():
+        filled(recv2.at[cols - 1, pl.ds(0, near)], r2_sem.at[cols - 1])
+        finish(cols - 1, here, near + 1)
+
+    def last_and_near(j, carry):
+        @pl.when(j == cols - 2)
+        def _():
+            finish_near()
+        return last(j, carry)
+
+    lax.fori_loop(0, cols - 1, last_and_near, 0)
+    if cols == 1:
+        finish_near()
     filled(recv2.at[cols - 1, pl.ds(0, near + 1)], r2_sem.at[cols])
     finish(cols - 1, near + 1 - here, near + 1)
 

time: 96.2 us -> 96 us (level)
  no operation moved by 1% of the time
where the time goes in v4:
time: 96 us; the launch traced here: 95.8 us
  Pallas kernels  93.8 us (98%)
  local copies, waits for them, and re-layouts  2.02 us (2%)
    pallas_call x1, Pallas kernels, shards(): pl.pallas_call(functools.partial(kernel, wide, pair), out_shape=jax.Shape...  93.8 us
    unnamed x1, local copies, waits for them, and re-layouts  2.02 us

profile of v4, /device:TPU:14, one launch (start us, length us, event | category | flops | bytes accessed | tf_op | source)
XLA Modules:
  0.0 95.8 jit_solution(10924502225528219820)
XLA Ops:
  0.0 93.8 %shard_map.46 = f32[8,4,2,2,32,256]{5,4,3,2,1,0:T(8,128)S(1)} custom-call(bf16[8,4,2,2,32,256]{5,4,3,2,1,0:T(8,128)(2,1)} %bitcast.8, bf16[8,2,2,128,2,256]{5,4,3,2,1,0:T(2,128)(2,1)} %g_ref.1, f32[8,8]{1,0:T(8,128)} %bitcast.9, s32[1,8]{1,0:T(1,128)} %bits_hbm.1), custom_call_target="tpu_custom_call" | custom-call | tf_op jit(solution)/shard_map/pallas_call | solution.py:353
  93.8 2.0 %copy.6 = f32[1,32,2,2,32,256]{5,4,3,2,1,0:T(8,128)} copy(f32[1,32,2,2,32,256]{5,4,3,2,1,0:T(8,128)S(1)} %bitcast.7) | data formatting | bytes 8388608

commit v5 on v4

--- a/solution.py
+++ b/solution.py
@@ -18,7 +18,50 @@
     return lax.dot_general(a, b, (dims, ((), ())), preferred_element_type=F32)
 
 
-def kernel(wide, pair, x_ref, g_ref, proj_hbm, bits_hbm, out_ref,
+def scaled(prod, sr, si, put):
+    re = prod[0][0] - prod[1][1]
+    im = prod[0][1] + prod[1][0]
+    put(0, value=sr * re - si * im)
+    put(1, value=sr * im + si * re)
+
+
+def finish_late(wide, done_ref, late_ref, weight_ref, scale_ref, out_ref, result, sem, late_sem):
+    cols, count = done_ref.shape[1], late_ref.shape[0]
+    vch, width = late_ref.shape[3], late_ref.shape[4]
+    here = jnp.where(lax.axis_index("wide") < count, 0, count)
+    there = count - here
+
+    def whole(j):
+        return pltpu.make_async_copy(done_ref.at[:, j], out_ref.at[:, j], sem.at[j])
+
+    def mine():
+        part = pl.ds(here, count)
+        return pltpu.make_async_copy(done_ref.at[part, cols - 1], out_ref.at[part, cols - 1], sem.at[cols - 1])
+
+    def late():
+        return pltpu.make_async_copy(result, out_ref.at[pl.ds(there, count), cols - 1], late_sem)
+
+    for j in range(cols - 1):
+        whole(j).start()
+    mine().start()
+    lhs = [jnp.concatenate([late_ref[:, p, h].reshape(count * vch, width) for h in range(2)], axis=1)
+           for p in range(2)]
+    for g in range(2):
+        weight = [weight_ref[p, g].reshape(-1, width) for p in range(2)]
+        prod = [[dot(lhs[p], weight[t], ((1,), (0,))) for t in range(2)] for p in range(2)]
+
+        def put(p, value):
+            result[:, p, g] = value.reshape(count, vch, width)
+
+        scaled(prod, scale_ref[g, 0], scale_ref[g, 1], put)
+    late().start()
+    for j in range(cols - 1):
+        whole(j).wait()
+    mine().wait()
+    late().wait()
+
+
+def kernel(wide, pair, x_ref, g_ref, proj_hbm, bits_hbm, out_ref, late_ref, weight_ref, scale_ref,
            proj_ref, bits_ref, xs, raw, branch, recv1, send2, recv2, state,
            c_sem, x_sem, g_out, g_in, s1_sem, r1_sem, s2_sem, r2_sem, side_sem, out_know, in_know):
     me = lax.axis_index("wide")
@@ -237,11 +280,7 @@
             else:
                 axis = 1 if form == "rows" else 0
                 prod = [[dot(lhs[p], weight[t], ((axis,), (0,))) for t in range(2)] for p in range(2)]
-            re = prod[0][0] - prod[1][1]
-            im = prod[0][1] + prod[1][0]
-            sr, si = select(s, g)
-            put(0, g, sr * re - si * im)
-            put(1, g, sr * im + si * re)
+            scaled(prod, *select(s, g), functools.partial(put, g=g))
 
     def gathered(buf, j, start, count):
         part = pl.ds(start, count)
@@ -329,8 +368,12 @@
     lax.fori_loop(0, cols - 1, last_and_near, 0)
     if cols == 1:
         finish_near()
+    weight_ref[...] = branch[steps - 1]
+    for g in range(2):
+        for i, value in enumerate(select(steps - 1, g)):
+            scale_ref[g, i] = jnp.full(scale_ref.shape[2:], value, F32)
     filled(recv2.at[cols - 1, pl.ds(0, near + 1)], r2_sem.at[cols])
-    finish(cols - 1, near + 1 - here, near + 1)
+    late_ref[...] = recv2[cols - 1, pl.ds(near + 1 - here, near + 1)]
 
     filled(send2.at[:, pl.ds(0, wide - 1)], s1_sem)
     filled(send2.at[:, pl.ds(0, wide - 1)], s2_sem)
@@ -350,11 +393,14 @@
         dma = pltpu.SemaphoreType.DMA
         chunk = (cols, wide, parts, shared, vch, width)
         chunk_out = (wide, cols, parts, shared, vch, width)
-        out = pl.pallas_call(
+        late = (wide // 2, parts, shared, vch, width)
+        last = (parts, shared, shared, half * pair, width)
+        ends = pl.pallas_call(
             functools.partial(kernel, wide, pair),
-            out_shape=jax.ShapeDtypeStruct(chunk_out, F32),
+            out_shape=[jax.ShapeDtypeStruct(chunk_out, F32), jax.ShapeDtypeStruct(late, BF16),
+                       jax.ShapeDtypeStruct(last, BF16), jax.ShapeDtypeStruct((2, 2, 1, width), F32)],
             in_specs=[pl.BlockSpec(memory_space=pltpu.HBM)] * 4,
-            out_specs=pl.BlockSpec(memory_space=pltpu.VMEM),
+            out_specs=[pl.BlockSpec(memory_space=pltpu.VMEM)] * 4,
             scratch_shapes=[
                 pltpu.SMEM(proj.shape, F32),
                 pltpu.SMEM(bits.shape, jnp.int32),
@@ -374,6 +420,14 @@
             compiler_params=pltpu.CompilerParams(
                 collective_id=0, has_side_effects=True, vmem_limit_bytes=44 * 1024 * 1024),
         )(*(pltpu.with_memory_space_constraint(a, pltpu.HBM) for a in (x, branches, proj, bits)))
+        out = pl.pallas_call(
+            functools.partial(finish_late, wide),
+            out_shape=jax.ShapeDtypeStruct(chunk_out, F32),
+            in_specs=[pl.BlockSpec(memory_space=pltpu.VMEM)] * 4,
+            out_specs=pl.BlockSpec(memory_space=pltpu.HBM),
+            scratch_shapes=[pltpu.VMEM((wide // 2, parts, shared, vch, width), F32), dma((cols,)), dma(())],
+            compiler_params=pltpu.CompilerParams(vmem_limit_bytes=16 * 1024 * 1024),
+        )(*(pltpu.with_memory_space_constraint(a, pltpu.VMEM) for a in ends))
         return out.reshape(1, columns, parts, shared, vch, width)
 
     in_specs = (

time: 96 us -> 95.7 us (level)
  local copies, waits for them, and re-layouts: 2.02 us -> 0 us
  Pallas kernels: 93.8 us -> 95.5 us
    unnamed x1 -> x0, local copies, waits for them, and re-layouts: 2.02 us -> none
    pallas_call x1 -> x2, Pallas kernels: 93.8 us -> 95.5 us  [the longest x1 93.4 us: shards(): pl.pallas_call(functools.partial(kernel, wide, pair), out_shape=[jax.Shap...]
where the time goes in v5:
time: 95.7 us; the launch traced here: 95.5 us
  Pallas kernels  95.5 us (100%)
    pallas_call x1, Pallas kernels, shards(): pl.pallas_call(functools.partial(kernel, wide, pair), out_shape=[jax.Shap...  93.4 us
    pallas_call x1, Pallas kernels, shards(): pl.pallas_call(functools.partial(finish_late, wide), out_shape=jax.ShapeD...  2.06 us

profile of v5, /device:TPU:14, one launch (start us, length us, event | category | flops | bytes accessed | tf_op | source)
XLA Modules:
  0.0 95.5 jit_solution(1259914343373316351)
XLA Ops:
  0.0 93.4 %shard_map.46 = (f32[8,4,2,2,32,256]{5,4,3,2,1,0:T(8,128)S(1)}, bf16[4,2,2,32,256]{4,3,2,1,0:T(8,128)(2,1)S(1)}, bf16[2,2,2,256,256]{4,3,2,1,0:T(8,128)(2,1)S(1)}, f32[2,2,1,256]{3,2,1,0:T(1,128)S(1)}) custom-call(bf16[8,4,2,2,32,256]{5,4,3,2,1,0:T(8,128)(2,1)} %bitcast.7, bf16[8,2,2,128,2,256]{5,4,3,2,1,0:T(2,128)(2,1)} %g_ref.1, f32[8,8]{1,0:T(8,128)} %bitcast.8, ...), custom_call_target="tpu_custom_call" | custom-call | tf_op jit(solution)/shard_map/pallas_call | solution.py:398
  93.5 2.1 %shard_map.47 = f32[8,4,2,2,32,256]{5,4,3,2,1,0:T(8,128)} custom-call(f32[8,4,2,2,32,256]{5,4,3,2,1,0:T(8,128)S(1)} %get-tuple-element.9.done_ref, bf16[4,2,2,32,256]{4,3,2,1,0:T(8,128)(2,1)S(1)} %get-tuple-element.10.late_ref, bf16[2,2,2,256,256]{4,3,2,1,0:T(8,128)(2,1)S(1)} %get-tuple-element.11.weight_ref, f32[2,2,1,256]{3,2,1,0:T(1,128)S(1)} %get-tuple-element.12.scale_ref), custom_call_target="tpu_custom_call" | custom-call | tf_op jit(solution)/shard_map/pallas_call | solution.py:423

commit v6 on v5

--- a/solution.py
+++ b/solution.py
@@ -177,13 +177,6 @@
     for j in range(1, min(cols, 2)):
         first(j, device(row + inward, lane)).start()
 
-    def send_branch(s, carry):
-        keep(s).start()
-        for k in range(1, pair):
-            share(s, k).start()
-        return carry
-
-    lax.fori_loop(0, steps, send_branch, 0)
     for j in range(cols):
         first_own(j).start()
 
@@ -252,6 +245,13 @@
             else:
                 first(j, p).start()
 
+    def send_branch(s, carry):
+        keep(s).start()
+        for k in range(1, pair):
+            share(s, k).start()
+        return carry
+
+    lax.fori_loop(0, steps, send_branch, 0)
     for c in consts:
         c.wait()
 
@@ -342,6 +342,11 @@
 
     lax.fori_loop(0, cols, column, 0)
 
+    weight_ref[...] = branch[steps - 1]
+    for g in range(2):
+        for i, value in enumerate(select(steps - 1, g)):
+            scale_ref[g, i] = jnp.full(scale_ref.shape[2:], value, F32)
+
     def finish(j, start, count):
         def put_out(p, g, value):
             out_ref[pl.ds(start, count), j, p, g] = value.reshape(count, vch, width)
@@ -368,10 +373,6 @@
     lax.fori_loop(0, cols - 1, last_and_near, 0)
     if cols == 1:
         finish_near()
-    weight_ref[...] = branch[steps - 1]
-    for g in range(2):
-        for i, value in enumerate(select(steps - 1, g)):
-            scale_ref[g, i] = jnp.full(scale_ref.shape[2:], value, F32)
     filled(recv2.at[cols - 1, pl.ds(0, near + 1)], r2_sem.at[cols])
     late_ref[...] = recv2[cols - 1, pl.ds(near + 1 - here, near + 1)]
 

time: 95.7 us -> 95.6 us (level)
  no operation moved by 1% of the time
where the time goes in v6:
time: 95.6 us; the launch traced here: 95.4 us
  Pallas kernels  95.4 us (100%)
    pallas_call x1, Pallas kernels, shards(): pl.pallas_call(functools.partial(kernel, wide, pair), out_shape=[jax.Shap...  93.4 us
    pallas_call x1, Pallas kernels, shards(): pl.pallas_call(functools.partial(finish_late, wide), out_shape=jax.ShapeD...  2.06 us

profile of v6, /device:TPU:14, one launch (start us, length us, event | category | flops | bytes accessed | tf_op | source)
XLA Modules:
  0.0 95.4 jit_solution(9818202897350802906)
XLA Ops:
  0.0 93.4 %shard_map.46 = (f32[8,4,2,2,32,256]{5,4,3,2,1,0:T(8,128)S(1)}, bf16[4,2,2,32,256]{4,3,2,1,0:T(8,128)(2,1)S(1)}, bf16[2,2,2,256,256]{4,3,2,1,0:T(8,128)(2,1)S(1)}, f32[2,2,1,256]{3,2,1,0:T(1,128)S(1)}) custom-call(bf16[8,4,2,2,32,256]{5,4,3,2,1,0:T(8,128)(2,1)} %bitcast.7, bf16[8,2,2,128,2,256]{5,4,3,2,1,0:T(2,128)(2,1)} %g_ref.1, f32[8,8]{1,0:T(8,128)} %bitcast.8, ...), custom_call_target="tpu_custom_call" | custom-call | tf_op jit(solution)/shard_map/pallas_call | solution.py:399
  93.4 2.1 %shard_map.47 = f32[8,4,2,2,32,256]{5,4,3,2,1,0:T(8,128)} custom-call(f32[8,4,2,2,32,256]{5,4,3,2,1,0:T(8,128)S(1)} %get-tuple-element.9.done_ref, bf16[4,2,2,32,256]{4,3,2,1,0:T(8,128)(2,1)S(1)} %get-tuple-element.10.late_ref, bf16[2,2,2,256,256]{4,3,2,1,0:T(8,128)(2,1)S(1)} %get-tuple-element.11.weight_ref, f32[2,2,1,256]{3,2,1,0:T(1,128)S(1)} %get-tuple-element.12.scale_ref), custom_call_target="tpu_custom_call" | custom-call | tf_op jit(solution)/shard_map/pallas_call | solution.py:424

commit v7 on v6

--- a/solution.py
+++ b/solution.py
@@ -342,6 +342,9 @@
 
     lax.fori_loop(0, cols, column, 0)
 
+    filled(send2.at[:, pl.ds(0, wide - 1)], s1_sem)
+    for k in range(1, pair):
+        filled(raw.at[:, :, :, pl.ds(0, half)], g_out)
     weight_ref[...] = branch[steps - 1]
     for g in range(2):
         for i, value in enumerate(select(steps - 1, g)):
@@ -376,10 +379,7 @@
     filled(recv2.at[cols - 1, pl.ds(0, near + 1)], r2_sem.at[cols])
     late_ref[...] = recv2[cols - 1, pl.ds(near + 1 - here, near + 1)]
 
-    filled(send2.at[:, pl.ds(0, wide - 1)], s1_sem)
     filled(send2.at[:, pl.ds(0, wide - 1)], s2_sem)
-    for k in range(1, pair):
-        filled(raw.at[:, :, :, pl.ds(0, half)], g_out)
 
 
 def solution(mesh):

time: 95.6 us -> 95.6 us (level)
  no operation moved by 1% of the time
where the time goes in v7:
time: 95.6 us; the launch traced here: 95.4 us
  Pallas kernels  95.4 us (100%)
    pallas_call x1, Pallas kernels, shards(): pl.pallas_call(functools.partial(kernel, wide, pair), out_shape=[jax.Shap...  93.4 us
    pallas_call x1, Pallas kernels, shards(): pl.pallas_call(functools.partial(finish_late, wide), out_shape=jax.ShapeD...  2.06 us

profile of v7, /device:TPU:14, one launch (start us, length us, event | category | flops | bytes accessed | tf_op | source)
XLA Modules:
  0.0 95.4 jit_solution(13279286961314084730)
XLA Ops:
  0.0 93.4 %shard_map.46 = (f32[8,4,2,2,32,256]{5,4,3,2,1,0:T(8,128)S(1)}, bf16[4,2,2,32,256]{4,3,2,1,0:T(8,128)(2,1)S(1)}, bf16[2,2,2,256,256]{4,3,2,1,0:T(8,128)(2,1)S(1)}, f32[2,2,1,256]{3,2,1,0:T(1,128)S(1)}) custom-call(bf16[8,4,2,2,32,256]{5,4,3,2,1,0:T(8,128)(2,1)} %bitcast.7, bf16[8,2,2,128,2,256]{5,4,3,2,1,0:T(2,128)(2,1)} %g_ref.1, f32[8,8]{1,0:T(8,128)} %bitcast.8, ...), custom_call_target="tpu_custom_call" | custom-call | tf_op jit(solution)/shard_map/pallas_call | solution.py:399
  93.4 2.1 %shard_map.47 = f32[8,4,2,2,32,256]{5,4,3,2,1,0:T(8,128)} custom-call(f32[8,4,2,2,32,256]{5,4,3,2,1,0:T(8,128)S(1)} %get-tuple-element.9.done_ref, bf16[4,2,2,32,256]{4,3,2,1,0:T(8,128)(2,1)S(1)} %get-tuple-element.10.late_ref, bf16[2,2,2,256,256]{4,3,2,1,0:T(8,128)(2,1)S(1)} %get-tuple-element.11.weight_ref, f32[2,2,1,256]{3,2,1,0:T(1,128)S(1)} %get-tuple-element.12.scale_ref), custom_call_target="tpu_custom_call" | custom-call | tf_op jit(solution)/shard_map/pallas_call | solution.py:424
